TPU v7x, 32 devices: a whole 2x2x4 slice. The times are simulated.
32 devices in a mesh: rp: 2 (over x), pb: 16 (over z, y, core).
Axes of the slice: x: 2, y: 2, z: 4, core: 2. Of those that a mesh axis runs over, the one named last changes fastest.
Arguments:
- wannier_g: bfloat16 [2, 1024, 32, 1152], P(None, 'rp', 'pb'), may hold values from -0.19921875 to 0.19921875
- rp_coords: int32 [3, 1024], replicated, may hold values from -8 to 8
- q_coords: int32 [3, 64], P(None, ('rp', 'pb')), may hold values from 0 to 15
- k_index: int32 [1], replicated, may hold values from 0 to 7
- k_vectors: bfloat16 [8, 2, 32, 32], replicated, may hold values from -0.75 to 0.75
- kq_vectors: bfloat16 [64, 2, 32, 32], P(('rp', 'pb')), may hold values from -0.75 to 0.75
- modes: bfloat16 [64, 2, 36, 36], P(('rp', 'pb')), may hold values from -0.75 to 0.75
Outputs:
- rotated: float32 [64, 2, 32, 1152], P(('rp', 'pb'))
All inputs are finite; a program needn't handle non-finite values.
Results may differ from a plain program's by a relative error of at most 0.0054.
Values may be sent and summed in bfloat16 or wider, within the bound.
A program may use at most 64 MiB of HBM per device.

v0:
```python
import functools

import jax
import jax.numpy as jnp
import numpy as np
from jax import lax
from jax.experimental import pallas as pl
from jax.experimental.pallas import tpu as pltpu
from jax.sharding import PartitionSpec as P

NK = 16
LANES = 128
MESH = pl.DeviceIdType.MESH
F32 = jnp.float32
BF16 = jnp.bfloat16
ODD = np.linalg.solve(
    np.array([[h, h**3, h**5, h**7] for h in (1.0, 2.0, 3.0, 4.0)]),
    np.sin(np.pi * np.arange(1, 5) / 8.0),
)


def dot(a, b, dims=((1,), (0,))):
    return lax.dot_general(a, b, (dims, ((), ())), preferred_element_type=F32)


def iota(shape, axis):
    return lax.broadcasted_iota(jnp.int32, shape, axis)


def picks(rows, cols, hit):
    return jnp.where(hit(iota((rows, cols), 0), iota((rows, cols), 1)), 1.0, 0.0).astype(BF16)


def wave(sixteenths):
    h = NK // 4 - NK * jnp.abs(sixteenths - jnp.floor(sixteenths + 0.5))
    s = h * h
    return h * (ODD[0] + s * (ODD[1] + s * (ODD[2] + s * ODD[3])))


def wrapped(a, b, size):
    c = a + b
    return jnp.where(c >= size, c - size, c)


def cuts(tiles):
    if tiles < 8:
        return [tiles]
    first, rest = 2, tiles - 2
    sizes = [first] + [rest // 3 + (k < rest % 3) for k in range(3)]
    return sizes


def kernel(
    cfg, g_hbm, rp_hbm, q_ref, k_ref, kv_hbm, v_hbm, e_hbm, o_ref,
    g_buf, rp_ref, kv_ref, v_ref, e_ref, qrow, q_all, xsend, xrecv, red, recv, w_buf, rmat, v_left,
    g_sem, in_sem, qs_sem, qr_sem, xs_sem, xr_sem, s_sem, r_sem,
):
    n_rp, n_pb, qd, local, M, cols, bands, nu, RB, paired = cfg
    n = n_rp * n_pb
    ip, ib = lax.axis_index("rp"), lax.axis_index("pb")
    me = ip * n_pb + ib
    depth = local * M
    half = n_pb * RB
    tiles = cols // LANES

    def to_all(act):
        for dp in range(n_rp):
            p = wrapped(ip, dp, n_rp)

            def one(db, c, p=p):
                act(p, wrapped(ib, db, n_pb))
                return c

            lax.fori_loop(1 if dp == 0 else 0, n_pb, one, 0)

    barrier = pltpu.get_barrier_semaphore()
    to_all(
        lambda p, b: pl.semaphore_signal(barrier, inc=1, device_id=(p, b), device_id_type=MESH)
    )

    inputs = [
        pltpu.make_async_copy(a, b, in_sem.at[k])
        for k, (a, b) in enumerate(
            ((rp_hbm, rp_ref), (kv_hbm, kv_ref), (v_hbm, v_ref), (e_hbm, e_ref))
        )
    ]
    for c in inputs:
        c.start()
    loads = []
    for t in range(tiles):
        lanes = pl.ds(LANES * t, LANES)
        src = g_hbm.at[:, :, :, lanes] if paired else g_hbm.at[:, lanes]
        loads.append(pltpu.make_async_copy(src, g_buf.at[t], g_sem.at[t]))
    for c in loads:
        c.start()

    lane = iota((1, LANES), 1)
    row = jnp.zeros((1, LANES), jnp.int32)
    for d in range(3):
        for j in range(qd):
            row = jnp.where(lane == d * qd + j, q_ref[j, d], row)
    qrow[...] = (row & (NK - 1)).astype(F32)
    q_all[me] = qrow[...]
    for c in inputs:
        c.wait()

    own = rp_ref[:, pl.ds(pl.multiple_of(ip * local, LANES), local)] & (NK - 1)
    spread = picks(local, depth, lambda a, b: a == b // M)
    own = dot((own.astype(F32) * (1.0 / NK)).astype(BF16), spread)
    which = iota((LANES, depth), 0) // qd
    big = jnp.zeros((LANES, depth), F32)
    for d in range(3):
        big = jnp.where(which == d, own[d : d + 1, :], big)
    rmat[...] = big.astype(BF16)

    slot = iota((bands, half), 1) % RB
    m_of = (iota((bands, half), 1) // RB) * M + slot % M
    pick_m = jnp.where(iota((bands, half), 0) == m_of, 1.0, 0.0).astype(BF16)
    real_in = (slot // M) % 2 == 0
    for q in range(qd):
        a_r, a_i = [dot(v_ref[q, c], pick_m, ((0,), (0,))) for c in range(2)]
        mine = slot // (2 * M) == q
        top = jnp.where(mine, jnp.where(real_in, a_r, a_i), 0.0)
        low = jnp.where(mine, jnp.where(real_in, -a_i, a_r), 0.0)
        v_left[2 * bands * q : 2 * bands * (q + 1), :] = jnp.concatenate([top, low], 0).astype(BF16)

    unit = kv_ref[k_ref[0]]
    of_band_t = picks(bands, cols, lambda b, a: (a >= nu * b) & (a < nu * b + nu))
    of_mode_t = picks(nu, cols, lambda b, a: (a - b + nu * bands) % nu == 0)
    u_right = [dot(unit[c], of_band_t).astype(BF16) for c in range(2)]
    e_right = [[dot(e_ref[q, :, c, :], of_mode_t).astype(BF16) for c in range(2)] for q in range(qd)]

    def combine(t):
        first = t * LANES
        of_band = picks(LANES, bands, lambda a, b: (a + first >= nu * b) & (a + first < nu * b + nu))
        of_mode = picks(LANES, nu, lambda a, b: (a + first - b + nu * bands) % nu == 0)
        ur, ui = [dot(of_band, m) for m in u_right]
        for q in range(qd):
            er, ei = [dot(of_mode, m) for m in e_right[q]]
            w_buf[q, 0, first : first + LANES, :] = (ur * er - ui * ei).astype(BF16)
            w_buf[q, 1, first : first + LANES, :] = (ur * ei + ui * er).astype(BF16)

    todo = list(range(tiles))

    def combine_some(most):
        for _ in range(min(most, len(todo))):
            combine(todo.pop(0))

    combine_some(0)

    pl.semaphore_wait(barrier, n - 1)

    def q_copy(p, b, slot_of):
        return pltpu.make_async_remote_copy(
            src_ref=qrow, dst_ref=q_all.at[slot_of], send_sem=qs_sem.at[p * n_pb + b],
            recv_sem=qr_sem.at[slot_of], device_id=(p, b), device_id_type=MESH,
        )

    to_all(lambda p, b: q_copy(p, b, me).start())
    combine_some(3)

    def q_done(p, b):
        q_copy(p, b, p * n_pb + b).wait_recv()
        q_copy(p, b, me).wait_send()

    to_all(q_done)

    coords = jnp.concatenate(
        [
            jnp.broadcast_to(q_all[pl.ds(wrapped(ip, dp, n_rp) * n_pb, n_pb)], (n_pb, RB, LANES))
            for dp in range(n_rp)
        ],
        axis=0,
    ).reshape(n * RB, LANES)
    slot = iota((n * RB, LANES), 0) % RB
    coords = jnp.where(iota((n * RB, LANES), 1) % qd == slot // (2 * M), coords, 0.0)
    turns = dot(coords.astype(BF16), rmat[...])
    slot = iota((n * RB, 1), 0) % RB
    imag = (slot // M) % 2 == 1
    keep = (slot % M) == (iota((1, depth), 1) % M)
    left = jnp.concatenate(
        [
            jnp.where(keep, wave(turns + shift), 0.0).astype(BF16)
            for shift in (jnp.where(imag, 0.75, 0.0), jnp.where(imag, 0.0, 0.25))
        ],
        axis=1,
    )

    sizes = cuts(tiles)
    firsts = [sum(sizes[:c]) for c in range(len(sizes))]
    lanes = [slice(LANES * a, LANES * (a + b)) for a, b in zip(firsts, sizes)]

    def x_copy(dp, c):
        part = (slice(None), slice(None), lanes[c])
        return pltpu.make_async_remote_copy(
            src_ref=xsend.at[(dp - 1, *part)], dst_ref=xrecv.at[(dp - 1, *part)],
            send_sem=xs_sem.at[dp - 1, c], recv_sem=xr_sem.at[dp - 1, c],
            device_id=(wrapped(ip, dp, n_rp), ib), device_id_type=MESH,
        )

    def f_copy(b, block, c):
        return pltpu.make_async_remote_copy(
            src_ref=red.at[b, :, lanes[c]], dst_ref=recv.at[block, :, lanes[c]],
            send_sem=s_sem.at[c, b], recv_sem=r_sem.at[c, block],
            device_id=(ip, b), device_id_type=MESH,
        )

    def to_group(act):
        def one(db, c):
            act(wrapped(ib, db, n_pb))
            return c

        lax.fori_loop(1, n_pb, one, 0)

    owned = {}

    def fourier(c):
        parts = []
        for u in range(firsts[c], firsts[c] + sizes[c]):
            loads[u].wait()
            parts.append(g_buf.at[u].reshape(2 * depth, LANES)[...] if paired else g_buf[u])
        right = parts[0] if len(parts) == 1 else jnp.concatenate(parts, axis=1)
        f = dot(left, right)
        owned[c] = f[:half]
        wide = LANES * sizes[c]
        for dp in range(1, n_rp):
            away = f[dp * half : (dp + 1) * half].astype(BF16)
            xsend[dp - 1, :, :, lanes[c]] = away.reshape(n_pb, RB, wide)
            x_copy(dp, c).start()

    def reduce(c):
        total = owned.pop(c)
        wide = LANES * sizes[c]
        for dp in range(1, n_rp):
            x_copy(dp, c).wait()
            total = total + xrecv[dp - 1, :, :, lanes[c]].astype(F32).reshape(half, wide)
        red[:, :, lanes[c]] = total.astype(BF16).reshape(n_pb, RB, wide)
        to_group(lambda b: f_copy(b, ib, c).start())
        recv[ib, :, lanes[c]] = red[ib, :, lanes[c]]

    count = len(sizes)
    fourier(0)
    for c in range(1, count):
        fourier(c)
        if c >= 2:
            reduce(c - 2)
    for c in range(max(count - 2, 0), count):
        combine_some(1 + (c == count - 1))
        reduce(c)
    combine_some(tiles)

    sums = [[0.0, 0.0] for _ in range(qd)]
    for c in range(count):

        def f_done(b, c=c):
            f_copy(b, b, c).wait_recv()
            f_copy(b, ib, c).wait_send()

        to_group(f_done)
        block = recv[:, :, lanes[c]].reshape(half, LANES * sizes[c])
        y = dot(v_left[...], block).astype(BF16)
        for q in range(qd):
            yq = y[2 * bands * q : 2 * bands * (q + 1)]
            for part in range(2):
                sums[q][part] = sums[q][part] + dot(yq, w_buf[q, part, lanes[c], :])
    for q in range(qd):
        a, b = sums[q]
        o_ref[q, 0] = a[:bands] - b[bands:]
        o_ref[q, 1] = a[bands:] + b[:bands]


def body(wannier_g, rp_coords, q_coords, k_index, k_vectors, kq_vectors, modes):
    n_rp, n_pb = lax.axis_size("rp"), lax.axis_size("pb")
    n = n_rp * n_pb
    qd = q_coords.shape[1]
    _, local, M, cols = wannier_g.shape
    bands, nu = kq_vectors.shape[2], modes.shape[2]
    RB = -(-(qd * 2 * M) // 8) * 8
    paired = M == 2
    tiles = cols // LANES
    chunks = len(cuts(tiles))
    right = wannier_g if paired else wannier_g.reshape(2 * local * M, cols)
    g_shape = (tiles, 2, local, M, LANES) if paired else (tiles, 2 * local * M, LANES)
    cfg = (n_rp, n_pb, qd, local, M, cols, bands, nu, RB, paired)
    hbm = pl.BlockSpec(memory_space=pltpu.HBM)
    smem = pl.BlockSpec(memory_space=pltpu.SMEM)
    modes = modes.transpose(0, 2, 1, 3)
    others = max(n_rp - 1, 1)
    return pl.pallas_call(
        functools.partial(kernel, cfg),
        out_shape=jax.ShapeDtypeStruct((qd, 2, bands, cols), F32),
        in_specs=[hbm, hbm, smem, smem, hbm, hbm, hbm],
        out_specs=pl.BlockSpec(memory_space=pltpu.VMEM),
        scratch_shapes=[
            pltpu.VMEM(g_shape, BF16),
            pltpu.VMEM(rp_coords.shape, jnp.int32),
            pltpu.VMEM(k_vectors.shape, BF16),
            pltpu.VMEM(kq_vectors.shape, BF16),
            pltpu.VMEM(modes.shape, BF16),
            pltpu.VMEM((1, LANES), F32),
            pltpu.VMEM((n, 1, LANES), F32),
            pltpu.VMEM((others, n_pb, RB, cols), BF16),
            pltpu.VMEM((others, n_pb, RB, cols), BF16),
            pltpu.VMEM((n_pb, RB, cols), BF16),
            pltpu.VMEM((n_pb, RB, cols), BF16),
            pltpu.VMEM((qd, 2, cols, cols), BF16),
            pltpu.VMEM((LANES, local * M), BF16),
            pltpu.VMEM((qd * 2 * bands, n_pb * RB), BF16),
            pltpu.SemaphoreType.DMA((tiles,)),
            pltpu.SemaphoreType.DMA((4,)),
            pltpu.SemaphoreType.DMA((n,)),
            pltpu.SemaphoreType.DMA((n,)),
            pltpu.SemaphoreType.DMA((others, chunks)),
            pltpu.SemaphoreType.DMA((others, chunks)),
            pltpu.SemaphoreType.DMA((chunks, n_pb)),
            pltpu.SemaphoreType.DMA((chunks, n_pb)),
        ],
        compiler_params=pltpu.CompilerParams(
            collective_id=0, has_side_effects=True, vmem_limit_bytes=60 * 2**20
        ),
    )(right, rp_coords, q_coords.T, k_index, k_vectors, kq_vectors, modes)


def solution(mesh):
    return jax.shard_map(
        body,
        mesh=mesh,
        in_specs=(
            P(None, "rp", "pb", None),
            P(),
            P(None, ("rp", "pb")),
            P(),
            P(),
            P(("rp", "pb"), None, None, None),
            P(("rp", "pb"), None, None, None),
        ),
        out_specs=P(("rp", "pb"), None, None, None),
        check_vma=False,
    )
```

profile of v0, /device:TPU:0, one launch (start us, length us, event | category | flops | bytes accessed | tf_op | source)
XLA Modules:
  0.0 33.8 jit_solution(15120369219207687664)
XLA Ops:
  0.7 31.3 %shard_map.73 = f32[2,2,32,1152]{3,2,1,0:T(8,128)} custom-call(bf16[2,512,2,1152]{3,2,1,0:T(2,128)(2,1)} %g_hbm.1, s32[3,1024]{1,0:T(4,128)} %rp_hbm.1, s32[2,3]{1,0:T(2,128)} %bitcast.3, s32[1]{0:T(128)S(6)} %copy.9.k_ref, bf16[8,2,32,32]{3,2,1,0:T(8,128)(2,1)} %kv_hbm.1, bf16[2,2,32,32]{3,2,1,0:T(8,128)(2,1)} %v_hbm.1, bf16[2,36,2,36]{3,2,1,0:T(2,128)(2,1)} %bitcast.2), custom_call_target="tpu_custom_call" | custom-call | tf_op jit(solution)/shard_map/pallas_call | solution.py:289
  31.9 1.9 %copy.10 = f32[2,2,32,1152]{3,2,1,0:T(8,128)} copy(f32[2,2,32,1152]{3,2,1,0:T(8,128)} %shard_map.73) | data formatting | bytes 1179648
where the time goes:
time: 34 us; the launch traced here: 33.8 us
  Pallas kernels  31.3 us (92%)
  local copies, waits for them, and re-layouts  1.92 us (6%)
  between operations  0.66 us (2%)
    pallas_call x1, Pallas kernels, body(): pl.pallas_call(functools.partial(kernel, cfg), out_shape=jax.ShapeDtypeSt...  31.3 us
    unnamed x1, local copies, waits for them, and re-layouts  1.92 us

commit v1 on v0

v1 whole, which is shorter than its diff:
```python
import functools

import jax
import jax.numpy as jnp
import numpy as np
from jax import lax
from jax.experimental import pallas as pl
from jax.experimental.pallas import tpu as pltpu
from jax.sharding import PartitionSpec as P

NK = 16
LANES = 128
MESH = pl.DeviceIdType.MESH
F32 = jnp.float32
BF16 = jnp.bfloat16
ROUND = 1.5 * 2.0**23 * NK
ODD = np.linalg.solve(
    np.array([[h, h**3, h**5, h**7] for h in (1.0, 2.0, 3.0, 4.0)]),
    np.sin(np.pi * np.arange(1, 5) / 8.0),
)


def dot(a, b, dims=((1,), (0,))):
    return lax.dot_general(a, b, (dims, ((), ())), preferred_element_type=F32)


def iota(shape, axis):
    return lax.broadcasted_iota(jnp.int32, shape, axis)


def picks(rows, cols, hit):
    return jnp.where(hit(iota((rows, cols), 0), iota((rows, cols), 1)), 1.0, 0.0).astype(BF16)


def wave(t):
    h = NK // 4 - jnp.abs(t - ((t + ROUND) - ROUND))
    s = h * h
    return h * (ODD[0] + s * (ODD[1] + s * (ODD[2] + s * ODD[3])))


def wrapped(a, b, size):
    c = a + b
    return jnp.where(c >= size, c - size, c)


def cuts(tiles):
    if tiles < 8:
        return [tiles]
    rest = tiles - 2
    return [1] + [rest // 3 + (k == 1) * (rest % 3) for k in range(3)] + [1]


def kernel(
    cfg, g_hbm, rp_hbm, q_hbm, k_hbm, kv_hbm, v_hbm, e_hbm, o_ref,
    g_buf, q_ref, k_ref, rp_ref, kv_ref, v_ref, e_ref, qrow, q_all, xsend, xrecv, own_f, red, recv,
    w_buf, rmat, v_left,
    g_sem, in_sem, qs_sem, qr_sem, xs_sem, xr_sem, s_sem, r_sem,
):
    n_rp, n_pb, qd, local, M, cols, bands, nu, RB, KL, paired = cfg
    n = n_rp * n_pb
    ip, ib = lax.axis_index("rp"), lax.axis_index("pb")
    me = ip * n_pb + ib
    depth = local * M
    tiles = cols // LANES
    nh = n_pb // 2
    rows = nh * RB
    near0 = (ib // nh) * nh
    far0 = nh - near0
    starts = (far0, near0)

    def group(g, act):
        def one(k, c):
            act(wrapped(ib - near0, k, nh) + starts[g])
            return c

        lax.fori_loop(g, nh, one, 0)

    def to_all(act):
        for dp in range(1, n_rp):
            for g in range(2):
                p = wrapped(ip, dp, n_rp)
                if g == 1:
                    act(p, ib)
                group(g, lambda b, p=p: act(p, b))
        for g in range(2):
            group(g, lambda b: act(ip, b))

    barrier = pltpu.get_barrier_semaphore()
    to_all(
        lambda p, b: pl.semaphore_signal(barrier, inc=1, device_id=(p, b), device_id_type=MESH)
    )

    inputs = [
        pltpu.make_async_copy(a, b, in_sem.at[k])
        for k, (a, b) in enumerate(
            (
                (q_hbm, q_ref), (k_hbm, k_ref), (rp_hbm, rp_ref), (kv_hbm, kv_ref),
                (v_hbm, v_ref), (e_hbm, e_ref),
            )
        )
    ]
    for c in inputs:
        c.start()
    flat = g_hbm.reshape(2 * depth, cols) if paired else g_hbm
    for t in range(tiles):
        src = flat.at[:, pl.ds(LANES * t, LANES)]
        pltpu.make_async_copy(src, g_buf.at[t], g_sem).start()

    inputs[0].wait()
    lane = iota((1, LANES), 1)
    row = jnp.zeros((1, LANES), jnp.int32)
    for d in range(3):
        for j in range(qd):
            row = jnp.where(lane // M == d * qd + j, q_ref[j, d], row)
    qrow[...] = (row & (NK - 1)).astype(F32)
    q_all[me] = qrow[...]

    pl.semaphore_wait(barrier, n - 1)

    def q_copy(p, b, kind):
        return pltpu.make_async_remote_copy(
            src_ref=qrow, dst_ref=q_all.at[me], send_sem=qs_sem,
            recv_sem=qr_sem.at[kind], device_id=(p, b), device_id_type=MESH,
        )

    for dp in range(1, n_rp):
        p = wrapped(ip, dp, n_rp)
        group(0, lambda b, p=p: q_copy(p, b, 0).start())
    group(0, lambda b: q_copy(ip, b, 1).start())
    for dp in range(1, n_rp):
        p = wrapped(ip, dp, n_rp)
        q_copy(p, ib, 1).start()
        group(1, lambda b, p=p: q_copy(p, b, 1).start())
    group(1, lambda b: q_copy(ip, b, 1).start())
    partner = (wrapped(ip, 1 % n_rp, n_rp), ib)

    def q_waits(count, kind):
        part = q_all.at[pl.ds(0, count)]
        return pltpu.make_async_remote_copy(
            src_ref=part, dst_ref=part, send_sem=qs_sem, recv_sem=qr_sem.at[kind],
            device_id=partner, device_id_type=MESH,
        )

    for c in inputs[1:]:
        c.wait()

    own = rp_ref[:, pl.ds(pl.multiple_of(ip * local, LANES), local)] & (NK - 1)
    spread = picks(local, depth, lambda a, b: a == b // M)
    own = dot(own.astype(F32).astype(BF16), spread)
    at = iota((KL, depth), 0)
    same = at % M == iota((KL, depth), 1) % M
    which = at // (qd * M)
    big = jnp.zeros((KL, depth), F32)
    for d in range(3):
        big = jnp.where(which == d, own[d : d + 1, :], big)
    big = jnp.where(same, big, 0.0)
    first = 3 * qd * M
    part = (at - first) // M
    for c in range(2):
        turn = (0.0, 3.0 * NK / 4) if c == 0 else (NK / 4, 0.0)
        turn = jnp.where(same, jnp.where(part == 0, turn[0], turn[1]), NK / 4)
        turn = jnp.where(at < first + 2 * M, turn, 0.0)
        rmat[:, c * depth : (c + 1) * depth] = jnp.where(at < first, big, turn).astype(BF16)

    slot = iota((RB, LANES), 0)
    at = iota((RB, LANES), 1)
    takes = (at < first) & ((at // M) % qd == slot // (2 * M)) & (at % M == slot % M)
    const = jnp.where((slot < qd * 2 * M) & (at - first == slot % (2 * M)), 1.0, 0.0)

    half = n_pb * RB
    slot = iota((bands, half), 1) % RB
    m_of = (iota((bands, half), 1) // RB) * M + slot % M
    pick_m = jnp.where(iota((bands, half), 0) == m_of, 1.0, 0.0).astype(BF16)
    real_in = (slot // M) % 2 == 0
    for q in range(qd):
        a_r, a_i = [dot(v_ref[q, c], pick_m, ((0,), (0,))) for c in range(2)]
        mine = slot // (2 * M) == q
        top = jnp.where(mine, jnp.where(real_in, a_r, a_i), 0.0)
        low = jnp.where(mine, jnp.where(real_in, -a_i, a_r), 0.0)
        v_left[4 * bands * q : 4 * bands * (q + 1), :] = jnp.concatenate(
            [top, low, -low, top], 0
        ).astype(BF16)

    unit = kv_ref[k_ref[0, 0]]
    of_band_t = picks(bands, cols, lambda b, a: (a >= nu * b) & (a < nu * b + nu))
    of_mode_t = picks(nu, cols, lambda b, a: (a - b + nu * bands) % nu == 0)
    u_right = [dot(unit[c], of_band_t).astype(BF16) for c in range(2)]
    e_right = [[dot(e_ref[q, :, c, :], of_mode_t).astype(BF16) for c in range(2)] for q in range(qd)]

    def combine(t):
        first = t * LANES
        of_band = picks(LANES, bands, lambda a, b: (a + first >= nu * b) & (a + first < nu * b + nu))
        of_mode = picks(LANES, nu, lambda a, b: (a + first - b + nu * bands) % nu == 0)
        ur, ui = [dot(of_band, m) for m in u_right]
        for q in range(qd):
            er, ei = [dot(of_mode, m) for m in e_right[q]]
            w_buf[q, 2 * first : 2 * first + LANES, :] = (ur * er - ui * ei).astype(BF16)
            w_buf[q, 2 * first + LANES : 2 * first + 2 * LANES, :] = (ur * ei + ui * er).astype(BF16)

    todo = list(range(tiles))

    def combine_some(most):
        for _ in range(min(most, len(todo))):
            combine(todo.pop(0))

    combine_some(5)

    def left(parts):
        coords = []
        for dp, g in parts:
            at = wrapped(ip, dp, n_rp) * n_pb + starts[g]
            c = jnp.broadcast_to(q_all[pl.ds(at, nh)], (nh, RB, LANES))
            coords.append(jnp.where(takes, c, const).reshape(rows, LANES))
        coords = coords[0] if len(coords) == 1 else jnp.concatenate(coords, axis=0)
        return wave(dot(coords[:, :KL].astype(BF16), rmat[...])).astype(BF16)

    sizes = cuts(tiles)
    count = len(sizes)
    firsts = [sum(sizes[:c]) for c in range(count)]
    lanes = [slice(LANES * a, LANES * (a + b)) for a, b in zip(firsts, sizes)]

    def right(c):
        parts = [g_buf[u] for u in range(firsts[c], firsts[c] + sizes[c])]
        return parts[0] if len(parts) == 1 else jnp.concatenate(parts, axis=1)

    def x_copy(dp, g, c):
        part = (pl.ds(g * nh, nh), slice(None), lanes[c])
        return pltpu.make_async_remote_copy(
            src_ref=xsend.at[(dp - 1, *part)], dst_ref=xrecv.at[(dp - 1, *part)],
            send_sem=xs_sem, recv_sem=xr_sem.at[dp - 1, g, c],
            device_id=(wrapped(ip, dp, n_rp), ib), device_id_type=MESH,
        )

    def send_x(dp, g, c, f):
        xsend[dp - 1, g * nh : (g + 1) * nh, :, lanes[c]] = f.reshape(nh, RB, LANES * sizes[c]).astype(BF16)
        x_copy(dp, g, c).start()

    q_waits((n_rp - 1) * nh, 0).wait_recv()
    away = [(dp, 0) for dp in range(1, n_rp)]
    rest = [(dp, 1) for dp in range(1, n_rp)] + [(0, 0), (0, 1)]
    ahead = left(away) if away else None
    pltpu.make_async_copy(g_buf, g_buf, g_sem).wait()
    for c in range(count):
        if away:
            f = dot(ahead, right(c))
            for k, (dp, g) in enumerate(away):
                send_x(dp, g, c, f[k * rows : (k + 1) * rows])

    q_waits(n - 1 - (n_rp - 1) * nh, 1).wait_recv()
    behind = left(rest)
    for c in range(count):
        f = dot(behind, right(c))
        for k, (dp, g) in enumerate(rest):
            block = f[k * rows : (k + 1) * rows]
            if dp == 0:
                own_f[g * nh : (g + 1) * nh, :, lanes[c]] = block.reshape(nh, RB, LANES * sizes[c])
            else:
                send_x(dp, g, c, block)

    def f_copy(b, src, c):
        return pltpu.make_async_remote_copy(
            src_ref=red.at[src, :, lanes[c]], dst_ref=recv.at[ib, :, lanes[c]],
            send_sem=s_sem, recv_sem=r_sem.at[c],
            device_id=(ip, b), device_id_type=MESH,
        )

    def reduce(g, c):
        part = (slice(g * nh, (g + 1) * nh), slice(None), lanes[c])
        total = own_f[part]
        for dp in range(1, n_rp):
            x_copy(dp, g, c).wait_recv()
            total = total + xrecv[(dp - 1, *part)].astype(F32)
        red[part] = total.astype(BF16)
        group(g, lambda b: f_copy(b, b - starts[g] + g * nh, c).start())
        if g == 1:
            recv[ib, :, lanes[c]] = red[nh + ib - near0, :, lanes[c]]

    combine_some(1)
    for c in range(count):
        reduce(0, c)
    combine_some(1)
    for c in range(count):
        reduce(1, c)
        if c % 2 == 0:
            combine_some(1)
    combine_some(tiles)

    sums = [0.0] * qd
    for c in range(count):
        part = (pl.ds(0, n_pb - 1), slice(None), lanes[c])
        pltpu.make_async_remote_copy(
            src_ref=red.at[part], dst_ref=recv.at[part], send_sem=s_sem, recv_sem=r_sem.at[c],
            device_id=partner, device_id_type=MESH,
        ).wait_recv()
        block = recv[:, :, lanes[c]].reshape(half, LANES * sizes[c])
        y = dot(v_left[...], block).astype(BF16)
        for q in range(qd):
            at = 4 * bands * q
            ya, yb = y[at : at + 2 * bands], y[at + 2 * bands : at + 4 * bands]
            pieces = []
            for t in range(sizes[c]):
                cut = slice(LANES * t, LANES * (t + 1))
                pieces += [ya[:, cut], yb[:, cut]]
            w = w_buf[q, 2 * LANES * firsts[c] : 2 * LANES * (firsts[c] + sizes[c]), :]
            sums[q] = sums[q] + dot(jnp.concatenate(pieces, axis=1), w)
    for q in range(qd):
        o_ref[q, 0] = sums[q][:bands]
        o_ref[q, 1] = sums[q][bands:]
    q_waits(n - 1, 0).wait_send()
    if n_rp > 1:
        pltpu.make_async_remote_copy(
            src_ref=xsend, dst_ref=xrecv, send_sem=xs_sem, recv_sem=xr_sem.at[0, 0, 0],
            device_id=partner, device_id_type=MESH,
        ).wait_send()
    part = pl.ds(0, n_pb - 1)
    pltpu.make_async_remote_copy(
        src_ref=red.at[part], dst_ref=recv.at[part], send_sem=s_sem, recv_sem=r_sem.at[0],
        device_id=partner, device_id_type=MESH,
    ).wait_send()


def body(wannier_g, rp_coords, q_coords, k_index, k_vectors, kq_vectors, modes):
    n_rp, n_pb = lax.axis_size("rp"), lax.axis_size("pb")
    n = n_rp * n_pb
    qd = q_coords.shape[1]
    _, local, M, cols = wannier_g.shape
    bands, nu = kq_vectors.shape[2], modes.shape[2]
    RB = -(-(qd * 2 * M) // 8) * 8
    KL = -(-(3 * qd * M + 2 * M) // 16) * 16
    tiles = cols // LANES
    chunks = len(cuts(tiles))
    paired = M == 2
    right = wannier_g if paired else wannier_g.reshape(2 * local * M, cols)
    cfg = (n_rp, n_pb, qd, local, M, cols, bands, nu, RB, KL, paired)
    hbm = pl.BlockSpec(memory_space=pltpu.HBM)
    modes = modes.transpose(0, 2, 1, 3)
    others = max(n_rp - 1, 1)
    return pl.pallas_call(
        functools.partial(kernel, cfg),
        out_shape=pltpu.VMEM((qd, 2, bands, cols), F32),
        in_specs=[hbm] * 7,
        out_specs=pl.BlockSpec(memory_space=pltpu.VMEM),
        scratch_shapes=[
            pltpu.VMEM((tiles, 2 * local * M, LANES), BF16),
            pltpu.SMEM((qd, 3), jnp.int32),
            pltpu.SMEM((1, 1), jnp.int32),
            pltpu.VMEM(rp_coords.shape, jnp.int32),
            pltpu.VMEM(k_vectors.shape, BF16),
            pltpu.VMEM(kq_vectors.shape, BF16),
            pltpu.VMEM(modes.shape, BF16),
            pltpu.VMEM((1, LANES), F32),
            pltpu.VMEM((n, 1, LANES), F32),
            pltpu.VMEM((others, n_pb, RB, cols), BF16),
            pltpu.VMEM((others, n_pb, RB, cols), BF16),
            pltpu.VMEM((n_pb, RB, cols), F32),
            pltpu.VMEM((n_pb, RB, cols), BF16),
            pltpu.VMEM((n_pb, RB, cols), BF16),
            pltpu.VMEM((qd, 2 * cols, cols), BF16),
            pltpu.VMEM((KL, 2 * local * M), BF16),
            pltpu.VMEM((qd * 4 * bands, n_pb * RB), BF16),
            pltpu.SemaphoreType.DMA,
            pltpu.SemaphoreType.DMA((6,)),
            pltpu.SemaphoreType.DMA,
            pltpu.SemaphoreType.DMA((2,)),
            pltpu.SemaphoreType.DMA,
            pltpu.SemaphoreType.DMA((others, 2, chunks)),
            pltpu.SemaphoreType.DMA,
            pltpu.SemaphoreType.DMA((chunks,)),
        ],
        compiler_params=pltpu.CompilerParams(
            collective_id=0, has_side_effects=True, vmem_limit_bytes=60 * 2**20
        ),
    )(right, rp_coords, q_coords.T, k_index.reshape(1, 1), k_vectors, kq_vectors, modes)


def solution(mesh):
    return jax.shard_map(
        body,
        mesh=mesh,
        in_specs=(
            P(None, "rp", "pb", None),
            P(),
            P(None, ("rp", "pb")),
            P(),
            P(),
            P(("rp", "pb"), None, None, None),
            P(("rp", "pb"), None, None, None),
        ),
        out_specs=P(("rp", "pb"), None, None, None),
        check_vma=False,
    )
```

time: 34 us -> 28.9 us (0.85)
  Pallas kernels: 31.3 us -> 27.2 us
  local copies, waits for them, and re-layouts: 1.92 us -> 0.82 us
    pallas_call x1, Pallas kernels: 31.3 us -> 27.2 us  [body(): pl.pallas_call(functools.partial(kernel, cfg), out_shape=pltpu.VMEM((qd,...]
    unnamed x1, local copies, waits for them, and re-layouts: 1.92 us -> 0.82 us
where the time goes in v1:
time: 28.9 us; the launch traced here: 28.7 us
  Pallas kernels  27.2 us (94%)
  local copies, waits for them, and re-layouts  0.82 us (3%)
  between operations  0.66 us (2%)
    pallas_call x1, Pallas kernels, body(): pl.pallas_call(functools.partial(kernel, cfg), out_shape=pltpu.VMEM((qd,...  27.2 us
    unnamed x1, local copies, waits for them, and re-layouts  0.82 us

profile of v1, /device:TPU:0, one launch (start us, length us, event | category | flops | bytes accessed | tf_op | source)
XLA Modules:
  0.0 28.7 jit_solution(9931939965515250237)
XLA Ops:
  0.7 27.2 %shard_map.73 = f32[2,2,32,1152]{3,2,1,0:T(8,128)S(1)} custom-call(bf16[2,512,2,1152]{3,2,1,0:T(2,128)(2,1)} %g_hbm.1, s32[3,1024]{1,0:T(4,128)} %rp_hbm.1, s32[2,3]{1,0:T(2,128)} %bitcast.5, s32[1,1]{1,0:T(1,128)} %bitcast.3.k_hbm, bf16[8,2,32,32]{3,2,1,0:T(8,128)(2,1)} %kv_hbm.1, bf16[2,2,32,32]{3,2,1,0:T(8,128)(2,1)} %v_hbm.1, bf16[2,36,2,36]{3,2,1,0:T(2,128)(2,1)} %bitcast.4), custom_call_target="tpu_custom_call" | custom-call | tf_op jit(solution)/shard_map/pallas_call | solution.py:338
  27.9 0.8 %copy.9 = f32[2,2,32,1152]{3,2,1,0:T(8,128)} copy(f32[2,2,32,1152]{3,2,1,0:T(8,128)S(1)} %shard_map.73) | data formatting | bytes 1179648

commit v2 on v1

--- a/solution.py
+++ b/solution.py
@@ -53,7 +53,7 @@
 def kernel(
     cfg, g_hbm, rp_hbm, q_hbm, k_hbm, kv_hbm, v_hbm, e_hbm, o_ref,
     g_buf, q_ref, k_ref, rp_ref, kv_ref, v_ref, e_ref, qrow, q_all, xsend, xrecv, own_f, red, recv,
-    w_buf, rmat, v_left,
+    e_buf, u_buf, rmat, v_left,
     g_sem, in_sem, qs_sem, qr_sem, xs_sem, xr_sem, s_sem, r_sem,
 ):
     n_rp, n_pb, qd, local, M, cols, bands, nu, RB, KL, paired = cfg
@@ -62,33 +62,36 @@
     me = ip * n_pb + ib
     depth = local * M
     tiles = cols // LANES
-    nh = n_pb // 2
-    rows = nh * RB
+    nh, nq = n_pb // 2, n_pb // 4
     near0 = (ib // nh) * nh
-    far0 = nh - near0
-    starts = (far0, near0)
+    quarter = ib // nq
+    starts = (((quarter + 2) % 4) * nq, (3 - quarter) * nq, near0)
+    sizes_of, offsets = (nq, nq, nh), (0, nq, nh)
+    OWN = 2
 
     def group(g, act):
+        size = sizes_of[g]
+
         def one(k, c):
-            act(wrapped(ib - near0, k, nh) + starts[g])
+            act(wrapped(ib % size, k, size) + starts[g])
             return c
 
-        lax.fori_loop(g, nh, one, 0)
-
-    def to_all(act):
+        lax.fori_loop(int(g == OWN), size, one, 0)
+
+    def to_kind(g, act):
         for dp in range(1, n_rp):
-            for g in range(2):
-                p = wrapped(ip, dp, n_rp)
-                if g == 1:
-                    act(p, ib)
-                group(g, lambda b, p=p: act(p, b))
-        for g in range(2):
-            group(g, lambda b: act(ip, b))
+            p = wrapped(ip, dp, n_rp)
+            if g == OWN:
+                act(p, ib)
+            group(g, lambda b, p=p: act(p, b))
+        group(g, lambda b: act(ip, b))
 
     barrier = pltpu.get_barrier_semaphore()
-    to_all(
-        lambda p, b: pl.semaphore_signal(barrier, inc=1, device_id=(p, b), device_id_type=MESH)
-    )
+    for g in range(3):
+        to_kind(
+            g,
+            lambda p, b: pl.semaphore_signal(barrier, inc=1, device_id=(p, b), device_id_type=MESH),
+        )
 
     inputs = [
         pltpu.make_async_copy(a, b, in_sem.at[k])
@@ -123,15 +126,8 @@
             recv_sem=qr_sem.at[kind], device_id=(p, b), device_id_type=MESH,
         )
 
-    for dp in range(1, n_rp):
-        p = wrapped(ip, dp, n_rp)
-        group(0, lambda b, p=p: q_copy(p, b, 0).start())
-    group(0, lambda b: q_copy(ip, b, 1).start())
-    for dp in range(1, n_rp):
-        p = wrapped(ip, dp, n_rp)
-        q_copy(p, ib, 1).start()
-        group(1, lambda b, p=p: q_copy(p, b, 1).start())
-    group(1, lambda b: q_copy(ip, b, 1).start())
+    for g in range(3):
+        to_kind(g, lambda p, b, g=g: q_copy(p, b, g).start())
     partner = (wrapped(ip, 1 % n_rp, n_rp), ib)
 
     def q_waits(count, kind):
@@ -177,40 +173,46 @@
         mine = slot // (2 * M) == q
         top = jnp.where(mine, jnp.where(real_in, a_r, a_i), 0.0)
         low = jnp.where(mine, jnp.where(real_in, -a_i, a_r), 0.0)
-        v_left[4 * bands * q : 4 * bands * (q + 1), :] = jnp.concatenate(
-            [top, low, -low, top], 0
-        ).astype(BF16)
-
+        v_left[2 * bands * q : 2 * bands * (q + 1), :] = jnp.concatenate([top, low], 0).astype(BF16)
+
+    def reach(t):
+        low, high = (LANES * t) // nu, (LANES * (t + 1) - 1) // nu
+        return (low * nu) // LANES, ((high + 1) * nu - 1) // LANES + 1
+
+    of_mode_t = picks(nu, cols, lambda b, a: (a - b + nu * bands) % nu == 0)
+    of_band_t = picks(bands, cols, lambda b, a: (a >= nu * b) & (a < nu * b + nu))
     unit = kv_ref[k_ref[0, 0]]
-    of_band_t = picks(bands, cols, lambda b, a: (a >= nu * b) & (a < nu * b + nu))
-    of_mode_t = picks(nu, cols, lambda b, a: (a - b + nu * bands) % nu == 0)
     u_right = [dot(unit[c], of_band_t).astype(BF16) for c in range(2)]
     e_right = [[dot(e_ref[q, :, c, :], of_mode_t).astype(BF16) for c in range(2)] for q in range(qd)]
-
-    def combine(t):
-        first = t * LANES
-        of_band = picks(LANES, bands, lambda a, b: (a + first >= nu * b) & (a + first < nu * b + nu))
-        of_mode = picks(LANES, nu, lambda a, b: (a + first - b + nu * bands) % nu == 0)
-        ur, ui = [dot(of_band, m) for m in u_right]
+    col = iota((1, cols), 1)
+    col_band, col_mode = col // nu, col % nu
+
+    for t in range(tiles):
+        lo, hi = reach(t)
+        span = slice(LANES * lo, LANES * hi)
+        rows_at = iota((LANES, 1), 0) + LANES * t
+        row_band = rows_at // nu
+        of_mode = picks(LANES, nu, lambda a, b: (a + LANES * t - b + nu * bands) % nu == 0)
+        diagonal = row_band == col_band[:, span]
         for q in range(qd):
-            er, ei = [dot(of_mode, m) for m in e_right[q]]
-            w_buf[q, 2 * first : 2 * first + LANES, :] = (ur * er - ui * ei).astype(BF16)
-            w_buf[q, 2 * first + LANES : 2 * first + 2 * LANES, :] = (ur * ei + ui * er).astype(BF16)
-
-    todo = list(range(tiles))
-
-    def combine_some(most):
-        for _ in range(min(most, len(todo))):
-            combine(todo.pop(0))
-
-    combine_some(5)
+            for c in range(2):
+                e = jnp.where(diagonal, dot(of_mode, e_right[q][c][:, span]), 0.0)
+                e_buf[q, (2 * t + c) * LANES : (2 * t + c + 1) * LANES, : LANES * (hi - lo)] = e.astype(BF16)
+
+    def spread_band(t):
+        rows_at = iota((LANES, 1), 0) + LANES * t
+        of_band = picks(LANES, bands, lambda a, b: (a + LANES * t >= nu * b) & (a + LANES * t < nu * b + nu))
+        diagonal = rows_at % nu == col_mode
+        for c in range(2):
+            u = jnp.where(diagonal, dot(of_band, u_right[c]), 0.0)
+            u_buf[(2 * t + c) * LANES : (2 * t + c + 1) * LANES, :] = u.astype(BF16)
 
     def left(parts):
         coords = []
         for dp, g in parts:
-            at = wrapped(ip, dp, n_rp) * n_pb + starts[g]
-            c = jnp.broadcast_to(q_all[pl.ds(at, nh)], (nh, RB, LANES))
-            coords.append(jnp.where(takes, c, const).reshape(rows, LANES))
+            at, size = wrapped(ip, dp, n_rp) * n_pb + starts[g], sizes_of[g]
+            c = jnp.broadcast_to(q_all[pl.ds(at, size)], (size, RB, LANES))
+            coords.append(jnp.where(takes, c, const).reshape(size * RB, LANES))
         coords = coords[0] if len(coords) == 1 else jnp.concatenate(coords, axis=0)
         return wave(dot(coords[:, :KL].astype(BF16), rmat[...])).astype(BF16)
 
@@ -224,38 +226,38 @@
         return parts[0] if len(parts) == 1 else jnp.concatenate(parts, axis=1)
 
     def x_copy(dp, g, c):
-        part = (pl.ds(g * nh, nh), slice(None), lanes[c])
+        part = (pl.ds(offsets[g], sizes_of[g]), slice(None), lanes[c])
         return pltpu.make_async_remote_copy(
             src_ref=xsend.at[(dp - 1, *part)], dst_ref=xrecv.at[(dp - 1, *part)],
             send_sem=xs_sem, recv_sem=xr_sem.at[dp - 1, g, c],
             device_id=(wrapped(ip, dp, n_rp), ib), device_id_type=MESH,
         )
 
-    def send_x(dp, g, c, f):
-        xsend[dp - 1, g * nh : (g + 1) * nh, :, lanes[c]] = f.reshape(nh, RB, LANES * sizes[c]).astype(BF16)
-        x_copy(dp, g, c).start()
-
-    q_waits((n_rp - 1) * nh, 0).wait_recv()
-    away = [(dp, 0) for dp in range(1, n_rp)]
-    rest = [(dp, 1) for dp in range(1, n_rp)] + [(0, 0), (0, 1)]
-    ahead = left(away) if away else None
-    pltpu.make_async_copy(g_buf, g_buf, g_sem).wait()
-    for c in range(count):
-        if away:
-            f = dot(ahead, right(c))
-            for k, (dp, g) in enumerate(away):
-                send_x(dp, g, c, f[k * rows : (k + 1) * rows])
-
-    q_waits(n - 1 - (n_rp - 1) * nh, 1).wait_recv()
-    behind = left(rest)
-    for c in range(count):
-        f = dot(behind, right(c))
-        for k, (dp, g) in enumerate(rest):
-            block = f[k * rows : (k + 1) * rows]
-            if dp == 0:
-                own_f[g * nh : (g + 1) * nh, :, lanes[c]] = block.reshape(nh, RB, LANES * sizes[c])
-            else:
-                send_x(dp, g, c, block)
+    def block_of(g, c):
+        return slice(offsets[g], offsets[g] + sizes_of[g]), slice(None), lanes[c]
+
+    def emit(g, c, f):
+        f = f.reshape(n_rp, sizes_of[g], RB, LANES * sizes[c])
+        for dp in range(1, n_rp):
+            xsend[(dp - 1, *block_of(g, c))] = f[dp - 1].astype(BF16)
+            x_copy(dp, g, c).start()
+        own_f[block_of(g, c)] = f[n_rp - 1]
+
+    def fourier(g, then):
+        count_of = n_rp * sizes_of[g] - (g == OWN)
+        q_waits(count_of, g).wait_recv()
+        phases = left([(dp, g) for dp in range(1, n_rp)] + [(0, g)])
+        if g == 0:
+            pltpu.make_async_copy(g_buf, g_buf, g_sem).wait()
+        held = None
+        for c in range(count):
+            f = dot(phases, right(c))
+            if held is not None:
+                emit(g, c - 1, held)
+                then(c - 1)
+            held = f
+        emit(g, count - 1, held)
+        then(count - 1)
 
     def f_copy(b, src, c):
         return pltpu.make_async_remote_copy(
@@ -265,27 +267,46 @@
         )
 
     def reduce(g, c):
-        part = (slice(g * nh, (g + 1) * nh), slice(None), lanes[c])
+        part = block_of(g, c)
         total = own_f[part]
         for dp in range(1, n_rp):
             x_copy(dp, g, c).wait_recv()
             total = total + xrecv[(dp - 1, *part)].astype(F32)
         red[part] = total.astype(BF16)
-        group(g, lambda b: f_copy(b, b - starts[g] + g * nh, c).start())
-        if g == 1:
-            recv[ib, :, lanes[c]] = red[nh + ib - near0, :, lanes[c]]
-
-    combine_some(1)
-    for c in range(count):
+        group(g, lambda b: f_copy(b, b - starts[g] + offsets[g], c).start())
+        if g == OWN:
+            recv[ib, :, lanes[c]] = red[offsets[g] + ib - near0, :, lanes[c]]
+
+    early = min(2, count)
+    fourier(0, lambda c: None)
+    fourier(1, lambda c: None)
+    for c in range(early):
         reduce(0, c)
-    combine_some(1)
+    fourier(2, lambda c: reduce(0, c) if c >= early else None)
     for c in range(count):
         reduce(1, c)
-        if c % 2 == 0:
-            combine_some(1)
-    combine_some(tiles)
-
-    sums = [0.0] * qd
+    todo = list(range(tiles))
+    for c in range(count):
+        for t in todo[: -(-tiles // count)]:
+            spread_band(t)
+        todo = todo[-(-tiles // count) :]
+        reduce(2, c)
+
+    def turned(z):
+        parts = []
+        for q in range(qd):
+            at = 2 * bands * q
+            parts += [-z[at + bands : at + 2 * bands], z[at : at + bands]]
+        return jnp.concatenate(parts, axis=0)
+
+    total = 0.0
+    carry = {}
+    done = 0
+    held = None
+
+    def by_band(total, pieces, at):
+        return total + dot(jnp.concatenate(pieces, axis=1), u_buf[at, :])
+
     for c in range(count):
         part = (pl.ds(0, n_pb - 1), slice(None), lanes[c])
         pltpu.make_async_remote_copy(
@@ -293,19 +314,38 @@
             device_id=partner, device_id_type=MESH,
         ).wait_recv()
         block = recv[:, :, lanes[c]].reshape(half, LANES * sizes[c])
-        y = dot(v_left[...], block).astype(BF16)
-        for q in range(qd):
-            at = 4 * bands * q
-            ya, yb = y[at : at + 2 * bands], y[at + 2 * bands : at + 4 * bands]
+        y = dot(v_left[...], block)
+        ya, yb = y.astype(BF16), turned(y).astype(BF16)
+        for t in range(firsts[c], firsts[c] + sizes[c]):
+            lo, hi = reach(t)
+            cut = slice(LANES * (t - firsts[c]), LANES * (t - firsts[c] + 1))
+            z = []
+            for q in range(qd):
+                at = slice(2 * bands * q, 2 * bands * (q + 1))
+                y_t = jnp.concatenate([ya[at, cut], yb[at, cut]], axis=1)
+                z.append(dot(y_t, e_buf[q, 2 * LANES * t : 2 * LANES * (t + 1), : LANES * (hi - lo)]))
+            z = jnp.concatenate(z, axis=0)
+            for u in range(lo, hi):
+                piece = z[:, LANES * (u - lo) : LANES * (u - lo + 1)]
+                carry[u] = carry[u] + piece if u in carry else piece
+        whole = LANES * (firsts[c] + sizes[c]) // nu * nu // LANES
+        ready = range(done, tiles if c == count - 1 else whole)
+        done = max(done, ready.stop)
+        if held is not None:
+            total = by_band(total, *held)
+            held = None
+        if len(ready):
             pieces = []
-            for t in range(sizes[c]):
-                cut = slice(LANES * t, LANES * (t + 1))
-                pieces += [ya[:, cut], yb[:, cut]]
-            w = w_buf[q, 2 * LANES * firsts[c] : 2 * LANES * (firsts[c] + sizes[c]), :]
-            sums[q] = sums[q] + dot(jnp.concatenate(pieces, axis=1), w)
+            for u in ready:
+                z = carry.pop(u)
+                pieces += [z.astype(BF16), turned(z).astype(BF16)]
+            at = slice(2 * LANES * ready.start, 2 * LANES * ready.stop)
+            held = pieces, at
+    total = by_band(total, *held)
     for q in range(qd):
-        o_ref[q, 0] = sums[q][:bands]
-        o_ref[q, 1] = sums[q][bands:]
+        for c in range(2):
+            at = bands * (2 * q + c)
+            o_ref[q, c] = total[at : at + bands]
     q_waits(n - 1, 0).wait_send()
     if n_rp > 1:
         pltpu.make_async_remote_copy(
@@ -355,15 +395,16 @@
             pltpu.VMEM((n_pb, RB, cols), F32),
             pltpu.VMEM((n_pb, RB, cols), BF16),
             pltpu.VMEM((n_pb, RB, cols), BF16),
-            pltpu.VMEM((qd, 2 * cols, cols), BF16),
+            pltpu.VMEM((qd, 2 * cols, LANES * (-(-LANES // nu) * nu // LANES + 2)), BF16),
+            pltpu.VMEM((2 * cols, cols), BF16),
             pltpu.VMEM((KL, 2 * local * M), BF16),
-            pltpu.VMEM((qd * 4 * bands, n_pb * RB), BF16),
+            pltpu.VMEM((qd * 2 * bands, n_pb * RB), BF16),
             pltpu.SemaphoreType.DMA,
             pltpu.SemaphoreType.DMA((6,)),
             pltpu.SemaphoreType.DMA,
-            pltpu.SemaphoreType.DMA((2,)),
+            pltpu.SemaphoreType.DMA((3,)),
             pltpu.SemaphoreType.DMA,
-            pltpu.SemaphoreType.DMA((others, 2, chunks)),
+            pltpu.SemaphoreType.DMA((others, 3, chunks)),
             pltpu.SemaphoreType.DMA,
             pltpu.SemaphoreType.DMA((chunks,)),
         ],

time: 28.9 us -> 26.3 us (0.910)
  Pallas kernels: 27.2 us -> 24.7 us
    pallas_call x1, Pallas kernels: 27.2 us -> 24.7 us  [body(): pl.pallas_call(functools.partial(kernel, cfg), out_shape=pltpu.VMEM((qd,...]
where the time goes in v2:
time: 26.3 us; the launch traced here: 26.2 us
  Pallas kernels  24.7 us (94%)
  local copies, waits for them, and re-layouts  0.82 us (3%)
  between operations  0.66 us (3%)
    pallas_call x1, Pallas kernels, body(): pl.pallas_call(functools.partial(kernel, cfg), out_shape=pltpu.VMEM((qd,...  24.7 us
    unnamed x1, local copies, waits for them, and re-layouts  0.82 us

profile of v2, /device:TPU:0, one launch (start us, length us, event | category | flops | bytes accessed | tf_op | source)
XLA Modules:
  0.0 26.2 jit_solution(14655071455531475295)
XLA Ops:
  0.7 24.7 %shard_map.73 = f32[2,2,32,1152]{3,2,1,0:T(8,128)S(1)} custom-call(bf16[2,512,2,1152]{3,2,1,0:T(2,128)(2,1)} %g_hbm.1, s32[3,1024]{1,0:T(4,128)} %rp_hbm.1, s32[2,3]{1,0:T(2,128)} %bitcast.5, s32[1,1]{1,0:T(1,128)} %bitcast.3.k_hbm, bf16[8,2,32,32]{3,2,1,0:T(8,128)(2,1)} %kv_hbm.1, bf16[2,2,32,32]{3,2,1,0:T(8,128)(2,1)} %v_hbm.1, bf16[2,36,2,36]{3,2,1,0:T(2,128)(2,1)} %bitcast.4), custom_call_target="tpu_custom_call" | custom-call | tf_op jit(solution)/shard_map/pallas_call | solution.py:378
  25.3 0.8 %copy.9 = f32[2,2,32,1152]{3,2,1,0:T(8,128)} copy(f32[2,2,32,1152]{3,2,1,0:T(8,128)S(1)} %shard_map.73) | data formatting | bytes 1179648

commit v3 on v2

--- a/solution.py
+++ b/solution.py
@@ -46,8 +46,7 @@
 def cuts(tiles):
     if tiles < 8:
         return [tiles]
-    rest = tiles - 2
-    return [1] + [rest // 3 + (k == 1) * (rest % 3) for k in range(3)] + [1]
+    return [2] * (tiles // 2) + [1] * (tiles % 2)
 
 
 def kernel(
@@ -62,34 +61,34 @@
     me = ip * n_pb + ib
     depth = local * M
     tiles = cols // LANES
-    nh, nq = n_pb // 2, n_pb // 4
-    near0 = (ib // nh) * nh
+    nq = n_pb // 4
     quarter = ib // nq
-    starts = (((quarter + 2) % 4) * nq, (3 - quarter) * nq, near0)
-    sizes_of, offsets = (nq, nq, nh), (0, nq, nh)
-    OWN = 2
-
-    def group(g, act):
-        size = sizes_of[g]
-
+    near = quarter + 1 - 2 * (quarter % 2)
+    starts = [q * nq for q in (quarter, (quarter + 2) % 4, near, 3 - quarter)]
+    blocks_of = ((0,), (1,), (2, 3))
+    KINDS = 3
+    OWN = 0
+
+    def to_block(j, act):
         def one(k, c):
-            act(wrapped(ib % size, k, size) + starts[g])
+            act(wrapped(ib % nq, k, nq) + starts[j])
             return c
 
-        lax.fori_loop(int(g == OWN), size, one, 0)
-
-    def to_kind(g, act):
-        for dp in range(1, n_rp):
-            p = wrapped(ip, dp, n_rp)
-            if g == OWN:
-                act(p, ib)
-            group(g, lambda b, p=p: act(p, b))
-        group(g, lambda b: act(ip, b))
+        lax.fori_loop(int(j == OWN), nq, one, 0)
+
+    def to_blocks(blocks, act):
+        for j in blocks:
+            for dp in range(1, n_rp):
+                p = wrapped(ip, dp, n_rp)
+                if j == OWN:
+                    act(p, ib)
+                to_block(j, lambda b, p=p: act(p, b))
+            to_block(j, lambda b: act(ip, b))
 
     barrier = pltpu.get_barrier_semaphore()
-    for g in range(3):
-        to_kind(
-            g,
+    for j in (3, 1, 2, 0):
+        to_blocks(
+            (j,),
             lambda p, b: pl.semaphore_signal(barrier, inc=1, device_id=(p, b), device_id_type=MESH),
         )
 
@@ -126,8 +125,8 @@
             recv_sem=qr_sem.at[kind], device_id=(p, b), device_id_type=MESH,
         )
 
-    for g in range(3):
-        to_kind(g, lambda p, b, g=g: q_copy(p, b, g).start())
+    for g in range(KINDS):
+        to_blocks(blocks_of[g], lambda p, b, g=g: q_copy(p, b, g).start())
     partner = (wrapped(ip, 1 % n_rp, n_rp), ib)
 
     def q_waits(count, kind):
@@ -209,10 +208,10 @@
 
     def left(parts):
         coords = []
-        for dp, g in parts:
-            at, size = wrapped(ip, dp, n_rp) * n_pb + starts[g], sizes_of[g]
-            c = jnp.broadcast_to(q_all[pl.ds(at, size)], (size, RB, LANES))
-            coords.append(jnp.where(takes, c, const).reshape(size * RB, LANES))
+        for dp, j in parts:
+            at = wrapped(ip, dp, n_rp) * n_pb + starts[j]
+            c = jnp.broadcast_to(q_all[pl.ds(at, nq)], (nq, RB, LANES))
+            coords.append(jnp.where(takes, c, const).reshape(nq * RB, LANES))
         coords = coords[0] if len(coords) == 1 else jnp.concatenate(coords, axis=0)
         return wave(dot(coords[:, :KL].astype(BF16), rmat[...])).astype(BF16)
 
@@ -226,7 +225,7 @@
         return parts[0] if len(parts) == 1 else jnp.concatenate(parts, axis=1)
 
     def x_copy(dp, g, c):
-        part = (pl.ds(offsets[g], sizes_of[g]), slice(None), lanes[c])
+        part = (pl.ds(nq * blocks_of[g][0], nq * len(blocks_of[g])), slice(None), lanes[c])
         return pltpu.make_async_remote_copy(
             src_ref=xsend.at[(dp - 1, *part)], dst_ref=xrecv.at[(dp - 1, *part)],
             send_sem=xs_sem, recv_sem=xr_sem.at[dp - 1, g, c],
@@ -234,30 +233,33 @@
         )
 
     def block_of(g, c):
-        return slice(offsets[g], offsets[g] + sizes_of[g]), slice(None), lanes[c]
+        return slice(nq * blocks_of[g][0], nq * (blocks_of[g][-1] + 1)), slice(None), lanes[c]
 
     def emit(g, c, f):
-        f = f.reshape(n_rp, sizes_of[g], RB, LANES * sizes[c])
+        f = f.reshape(n_rp, nq * len(blocks_of[g]), RB, LANES * sizes[c])
         for dp in range(1, n_rp):
             xsend[(dp - 1, *block_of(g, c))] = f[dp - 1].astype(BF16)
             x_copy(dp, g, c).start()
         own_f[block_of(g, c)] = f[n_rp - 1]
 
-    def fourier(g, then):
-        count_of = n_rp * sizes_of[g] - (g == OWN)
+    phases = {}
+
+    def phase(g):
+        count_of = n_rp * nq * len(blocks_of[g]) - (OWN in blocks_of[g])
         q_waits(count_of, g).wait_recv()
-        phases = left([(dp, g) for dp in range(1, n_rp)] + [(0, g)])
-        if g == 0:
-            pltpu.make_async_copy(g_buf, g_buf, g_sem).wait()
+        phases[g] = left([(dp, j) for dp in [*range(1, n_rp), 0] for j in blocks_of[g]])
+
+    def fourier(g, chunks, then=lambda c: None):
         held = None
-        for c in range(count):
-            f = dot(phases, right(c))
+        for c in chunks:
+            f = dot(phases[g], right(c))
             if held is not None:
-                emit(g, c - 1, held)
-                then(c - 1)
-            held = f
-        emit(g, count - 1, held)
-        then(count - 1)
+                emit(g, *held)
+                then(held[0])
+            held = c, f
+        if held is not None:
+            emit(g, *held)
+            then(held[0])
 
     def f_copy(b, src, c):
         return pltpu.make_async_remote_copy(
@@ -273,24 +275,33 @@
             x_copy(dp, g, c).wait_recv()
             total = total + xrecv[(dp - 1, *part)].astype(F32)
         red[part] = total.astype(BF16)
-        group(g, lambda b: f_copy(b, b - starts[g] + offsets[g], c).start())
-        if g == OWN:
-            recv[ib, :, lanes[c]] = red[offsets[g] + ib - near0, :, lanes[c]]
-
-    early = min(2, count)
-    fourier(0, lambda c: None)
-    fourier(1, lambda c: None)
-    for c in range(early):
-        reduce(0, c)
-    fourier(2, lambda c: reduce(0, c) if c >= early else None)
+        for j in blocks_of[g]:
+            to_block(j, lambda b, j=j: f_copy(b, b - starts[j] + nq * j, c).start())
+            if j == OWN:
+                recv[ib, :, lanes[c]] = red[nq * j + ib % nq, :, lanes[c]]
+
+    ahead = count - 2 if count > 2 else count
+    phase(0)
+    pltpu.make_async_copy(g_buf, g_buf, g_sem).wait()
+    fourier(0, range(ahead))
+    phase(1)
+    fourier(1, range(count))
+    fourier(0, range(ahead, count))
+    phase(2)
+    todo = [functools.partial(reduce, g, c) for g in (1, 0) for c in range(count)]
+    fourier(2, range(count), lambda c: todo.pop(0)() if c >= 2 else None)
+    for act in todo:
+        act()
+    bands_left = list(range(tiles))
+
+    def spread_some(most):
+        for _ in range(min(most, len(bands_left))):
+            spread_band(bands_left.pop(0))
+
     for c in range(count):
-        reduce(1, c)
-    todo = list(range(tiles))
-    for c in range(count):
-        for t in todo[: -(-tiles // count)]:
-            spread_band(t)
-        todo = todo[-(-tiles // count) :]
+        spread_some(4 if c == 0 else 1)
         reduce(2, c)
+    spread_some(tiles)
 
     def turned(z):
         parts = []

time: 26.3 us -> 25.8 us (0.981)
  Pallas kernels: 24.7 us -> 24.2 us
    pallas_call x1, Pallas kernels: 24.7 us -> 24.2 us  [body(): pl.pallas_call(functools.partial(kernel, cfg), out_shape=pltpu.VMEM((qd,...]
where the time goes in v3:
time: 25.8 us; the launch traced here: 25.7 us
  Pallas kernels  24.2 us (94%)
  local copies, waits for them, and re-layouts  0.82 us (3%)
  between operations  0.66 us (3%)
    pallas_call x1, Pallas kernels, body(): pl.pallas_call(functools.partial(kernel, cfg), out_shape=pltpu.VMEM((qd,...  24.2 us
    unnamed x1, local copies, waits for them, and re-layouts  0.82 us

profile of v3, /device:TPU:0, one launch (start us, length us, event | category | flops | bytes accessed | tf_op | source)
XLA Modules:
  0.0 25.7 jit_solution(2470198919169395104)
XLA Ops:
  0.7 24.2 %shard_map.73 = f32[2,2,32,1152]{3,2,1,0:T(8,128)S(1)} custom-call(bf16[2,512,2,1152]{3,2,1,0:T(2,128)(2,1)} %g_hbm.1, s32[3,1024]{1,0:T(4,128)} %rp_hbm.1, s32[2,3]{1,0:T(2,128)} %bitcast.5, s32[1,1]{1,0:T(1,128)} %bitcast.3.k_hbm, bf16[8,2,32,32]{3,2,1,0:T(8,128)(2,1)} %kv_hbm.1, bf16[2,2,32,32]{3,2,1,0:T(8,128)(2,1)} %v_hbm.1, bf16[2,36,2,36]{3,2,1,0:T(2,128)(2,1)} %bitcast.4), custom_call_target="tpu_custom_call" | custom-call | tf_op jit(solution)/shard_map/pallas_call | solution.py:389
  24.9 0.8 %copy.9 = f32[2,2,32,1152]{3,2,1,0:T(8,128)} copy(f32[2,2,32,1152]{3,2,1,0:T(8,128)S(1)} %shard_map.73) | data formatting | bytes 1179648

commit v4 on v3

--- a/solution.py
+++ b/solution.py
@@ -289,7 +289,7 @@
     fourier(0, range(ahead, count))
     phase(2)
     todo = [functools.partial(reduce, g, c) for g in (1, 0) for c in range(count)]
-    fourier(2, range(count), lambda c: todo.pop(0)() if c >= 2 else None)
+    fourier(2, range(count), lambda c: todo.pop(0)() if c >= 1 else None)
     for act in todo:
         act()
     bands_left = list(range(tiles))
@@ -310,20 +310,9 @@
             parts += [-z[at + bands : at + 2 * bands], z[at : at + bands]]
         return jnp.concatenate(parts, axis=0)
 
-    total = 0.0
     carry = {}
-    done = 0
-    held = None
-
-    def by_band(total, pieces, at):
-        return total + dot(jnp.concatenate(pieces, axis=1), u_buf[at, :])
-
-    for c in range(count):
-        part = (pl.ds(0, n_pb - 1), slice(None), lanes[c])
-        pltpu.make_async_remote_copy(
-            src_ref=red.at[part], dst_ref=recv.at[part], send_sem=s_sem, recv_sem=r_sem.at[c],
-            device_id=partner, device_id_type=MESH,
-        ).wait_recv()
+
+    def by_mode(c):
         block = recv[:, :, lanes[c]].reshape(half, LANES * sizes[c])
         y = dot(v_left[...], block)
         ya, yb = y.astype(BF16), turned(y).astype(BF16)
@@ -339,20 +328,34 @@
             for u in range(lo, hi):
                 piece = z[:, LANES * (u - lo) : LANES * (u - lo + 1)]
                 carry[u] = carry[u] + piece if u in carry else piece
-        whole = LANES * (firsts[c] + sizes[c]) // nu * nu // LANES
-        ready = range(done, tiles if c == count - 1 else whole)
-        done = max(done, ready.stop)
-        if held is not None:
-            total = by_band(total, *held)
-            held = None
-        if len(ready):
-            pieces = []
-            for u in ready:
-                z = carry.pop(u)
-                pieces += [z.astype(BF16), turned(z).astype(BF16)]
-            at = slice(2 * LANES * ready.start, 2 * LANES * ready.stop)
-            held = pieces, at
-    total = by_band(total, *held)
+
+    def by_band(first, last):
+        pieces = []
+        for u in range(first, last):
+            z = carry.pop(u)
+            pieces += [z.astype(BF16), turned(z).astype(BF16)]
+        return dot(jnp.concatenate(pieces, axis=1), u_buf[2 * LANES * first : 2 * LANES * last, :])
+
+    rounds = [[c] for c in range(count - 2)] + [list(range(max(count - 2, 0), count))]
+    total = 0.0
+    done = 0
+    whole = 0
+    for k, chunks in enumerate(rounds):
+        for c in chunks:
+            part = (pl.ds(0, n_pb - 1), slice(None), lanes[c])
+            pltpu.make_async_remote_copy(
+                src_ref=red.at[part], dst_ref=recv.at[part], send_sem=s_sem, recv_sem=r_sem.at[c],
+                device_id=partner, device_id_type=MESH,
+            ).wait_recv()
+        for c in chunks:
+            by_mode(c)
+        final = k == len(rounds) - 1
+        if not final:
+            whole = LANES * (firsts[chunks[-1]] + sizes[chunks[-1]]) // nu * nu // LANES
+        if whole > done and (final or (whole - done > 2 and k < len(rounds) - 2)):
+            total = total + by_band(done, whole)
+            done = whole
+    total = total + by_band(done, tiles)
     for q in range(qd):
         for c in range(2):
             at = bands * (2 * q + c)

time: 25.8 us -> 25.9 us (level)
  no operation moved by 1% of the time
where the time goes in v4:
time: 25.9 us; the launch traced here: 25.7 us
  Pallas kernels  24.2 us (93%)
  local copies, waits for them, and re-layouts  0.82 us (3%)
  between operations  0.66 us (3%)
    pallas_call x1, Pallas kernels, body(): pl.pallas_call(functools.partial(kernel, cfg), out_shape=pltpu.VMEM((qd,...  24.2 us
    unnamed x1, local copies, waits for them, and re-layouts  0.82 us

profile of v4, /device:TPU:0, one launch (start us, length us, event | category | flops | bytes accessed | tf_op | source)
XLA Modules:
  0.0 25.7 jit_solution(16845797236407077939)
XLA Ops:
  0.7 24.2 %shard_map.73 = f32[2,2,32,1152]{3,2,1,0:T(8,128)S(1)} custom-call(bf16[2,512,2,1152]{3,2,1,0:T(2,128)(2,1)} %g_hbm.1, s32[3,1024]{1,0:T(4,128)} %rp_hbm.1, s32[2,3]{1,0:T(2,128)} %bitcast.5, s32[1,1]{1,0:T(1,128)} %bitcast.3.k_hbm, bf16[8,2,32,32]{3,2,1,0:T(8,128)(2,1)} %kv_hbm.1, bf16[2,2,32,32]{3,2,1,0:T(8,128)(2,1)} %v_hbm.1, bf16[2,36,2,36]{3,2,1,0:T(2,128)(2,1)} %bitcast.4), custom_call_target="tpu_custom_call" | custom-call | tf_op jit(solution)/shard_map/pallas_call | solution.py:392
  24.9 0.8 %copy.9 = f32[2,2,32,1152]{3,2,1,0:T(8,128)} copy(f32[2,2,32,1152]{3,2,1,0:T(8,128)S(1)} %shard_map.73) | data formatting | bytes 1179648
